TPU v7x, 256 devices: a whole 4x4x8 slice. The times are simulated.
256 devices in a mesh: freq: 4 (over x_hi, core), rcv: 64 (over y, z, x_lo).
Axes of the slice: x: 4 (x_hi: 2, x_lo: 2; x = x_hi * 2 + x_lo), y: 4, z: 8, core: 2. Of those that a mesh axis runs over, the one named last changes fastest.
Arguments:
- reflection: bfloat16 [8, 2, 2560, 2560], P('freq', None, 'rcv'), may hold values from -5 to 5, as said below
- starts: int32 [2560, 192], P('rcv'), may hold values from 8 to 56
- focusing: float32 [8, 2560, 2, 192], P('freq', 'rcv'), may hold values from -6 to 6
- residual: float32 [8, 2560, 2, 192], P('freq', 'rcv'), may hold values from -6 to 6
- direction: float32 [8, 2560, 2, 192], P('freq', 'rcv'), may hold values from -6 to 6
- gradient: float32 [8, 2560, 2, 192], P('freq', 'rcv'), may hold values from -30 to 30
Outputs:
- new_focusing: float32 [8, 2560, 2, 192], P('freq', 'rcv')
- new_residual: float32 [8, 2560, 2, 192], P('freq', 'rcv')
- new_direction: float32 [8, 2560, 2, 192], P('freq', 'rcv')
- green_field: float32 [8, 2560, 2, 192], P('freq', 'rcv')
- focal_correlation: float32 [8, 2, 192], P('freq')
Inputs may be any that keep to these rules, and one draw needn't show every extreme that they name: Each frequency's matrix is symmetric in source and receiver: reflection[f, c, s, r] = reflection[f, c, r, s].
All inputs are finite; a program needn't handle non-finite values.
Results may differ from a plain program's by a relative error of at most 0.0003.
The roundings to bfloat16 on the way count: a program that leaves them out, or rounds other values in their place, can miss the bound.
Values may be sent and summed in bfloat16 or wider, within the bound.
A program may use at most 64 MiB of HBM per device.

v0:
```python
import math
import jax
import jax.numpy as jnp
from jax import lax
from jax.sharding import Mesh
from jax.sharding import PartitionSpec as P

N = 2560
F = 8
TS = 64
FREQ = ("freq_0", "freq_1")
RCV = ("rcv_0", "rcv_1", "rcv_2")
FREQ_RCV = ("freq_0", "freq_1", "rcv_0", "rcv_1", "rcv_2")
band_start = 5
tiny = 1e-06
highest = lax.Precision.HIGHEST


def in_order(pieces, dim):
    lengths = list(pieces.shape[1:])
    lengths[dim] *= pieces.shape[0]
    return jnp.moveaxis(pieces, 0, dim).reshape(lengths)


def sent_to_all(value, axis):
    count = lax.axis_size(axis)
    return lax.all_to_all(
        jnp.broadcast_to(value[None], (count, *value.shape)), axis, 0, 0, tiled=True
    )


def gather_directly(value, axis, dim):
    return in_order(sent_to_all(value, axis), dim)


def one_axis_at_a_time(value, axes):
    for axis in axes:
        value = lax.psum(value, axis)
    return value


def all_blocks(value, axes, sequence):
    pieces = value
    for k in sequence:
        pieces = lax.all_gather(pieces, axes[k])
    done = sequence[::-1]
    back = [done.index(k) for k in range(len(axes))]
    pieces = pieces.transpose(*back, *range(len(axes), pieces.ndim))
    return pieces.reshape(-1, *value.shape)


def gathered_by_axis(value, axes, sequence, dim):
    return in_order(all_blocks(value, axes, sequence), dim)


def of_everyone(value, axis):
    everything = sent_to_all(value, axis)
    return jnp.sum(everything, axis=0)


def tables(count, offset):
    times = jnp.arange(TS, dtype=jnp.float32)[:, None]
    bins = (jnp.arange(count, dtype=jnp.int32) + offset + band_start).astype(jnp.float32)[None, :]
    phase = 2.0 * jnp.pi * times * bins / TS
    return (jnp.cos(phase), jnp.sin(phase))


def contract_time(table, values):
    return jnp.einsum("tf,frk->trk", table, values, precision=highest)


def contract_back(table, values):
    return jnp.einsum("tf,trk->frk", table, values, precision=highest)


def time_gate(field, forward_cos, forward_sin, back_cos, back_sin, limits, complement):
    real_part = field[:, :, 0]
    imag_part = field[:, :, 1]
    time_real = contract_time(forward_cos, real_part) - contract_time(forward_sin, imag_part)
    time_imag = contract_time(forward_sin, real_part) + contract_time(forward_cos, imag_part)
    clock = jnp.arange(TS, dtype=jnp.int32)[:, None, None]
    window = (clock < limits[None]).astype(jnp.float32)
    if complement:
        window = 1.0 - window
    kept_real = window * time_real
    kept_imag = window * time_imag
    out_real = (contract_back(back_cos, kept_real) + contract_back(back_sin, kept_imag)) / TS
    out_imag = (contract_back(back_cos, kept_imag) - contract_back(back_sin, kept_real)) / TS
    return jnp.stack([out_real, out_imag], axis=2)


def combine(total, conjugate):
    if conjugate:
        out_real = total[:, 0, :, 0] + total[:, 1, :, 1]
        out_imag = total[:, 0, :, 1] - total[:, 1, :, 0]
    else:
        out_real = total[:, 0, :, 0] - total[:, 1, :, 1]
        out_imag = total[:, 0, :, 1] + total[:, 1, :, 0]
    return jnp.stack([out_real, out_imag], axis=2)


def per_device(reflection, starts, focusing, residual, direction, gradient):
    local_freq = reflection.shape[0]
    position = lax.axis_index(FREQ)
    cos_table, sin_table = tables(F, 0)
    own_cos, own_sin = tables(local_freq, position * local_freq)

    def gate(field, complement):
        whole = gather_directly(field, FREQ, 0)
        return time_gate(whole, cos_table, sin_table, own_cos, own_sin, starts, complement)

    def accumulate(piece):
        return jnp.einsum("fpnm,fmqk->fpnqk", reflection, piece, preferred_element_type=jnp.float32)

    direction_low = direction.astype(jnp.bfloat16)
    focusing_low = focusing.astype(jnp.bfloat16)
    aimed_total = accumulate(lax.all_gather(direction_low, RCV, axis=1, tiled=True))
    direction_image = combine(aimed_total, False)
    image = gate(direction_image, False)
    gamma, curvature = (
        one_axis_at_a_time(jnp.sum(gradient * gradient), FREQ_RCV),
        one_axis_at_a_time(jnp.sum(image * image), FREQ_RCV),
    )
    alpha = gamma / (curvature + tiny)
    new_focusing = focusing + alpha * direction
    new_residual = residual - alpha * image
    gated = gate(new_residual, False).astype(jnp.bfloat16)
    total = accumulate(gathered_by_axis(gated, RCV, (2, 0, 1), 1))
    new_gradient = combine(total, True)
    new_gamma = one_axis_at_a_time(jnp.sum(new_gradient * new_gradient), FREQ_RCV)
    new_direction = new_gradient + new_gamma / (gamma + tiny) * direction
    focus_total = accumulate(lax.all_gather(focusing_low, RCV, axis=1, tiled=True))
    focusing_image = combine(focus_total, False)
    green_field = gate(focusing_image + alpha * direction_image, True)
    corr_real = jnp.sum(
        green_field[:, :, 0] * new_focusing[:, :, 0] + green_field[:, :, 1] * new_focusing[:, :, 1],
        axis=1,
    )
    corr_imag = jnp.sum(
        green_field[:, :, 1] * new_focusing[:, :, 0] - green_field[:, :, 0] * new_focusing[:, :, 1],
        axis=1,
    )
    partial_corr = jnp.stack([corr_real, corr_imag], axis=1)
    focal_correlation = of_everyone(partial_corr, RCV) / math.sqrt(N)
    return (new_focusing, new_residual, new_direction, green_field, focal_correlation)


def solution(mesh):
    finer = Mesh(
        mesh.devices.reshape(2, 2, 4, 8, 2), ("freq_0", "freq_1", "rcv_0", "rcv_1", "rcv_2")
    )
    in_specs = (
        P(FREQ, None, RCV, None),
        P(RCV, None),
        P(FREQ, RCV, None, None),
        P(FREQ, RCV, None, None),
        P(FREQ, RCV, None, None),
        P(FREQ, RCV, None, None),
    )
    out_specs = (
        P(FREQ, RCV, None, None),
        P(FREQ, RCV, None, None),
        P(FREQ, RCV, None, None),
        P(FREQ, RCV, None, None),
        P(FREQ, None, None),
    )
    return jax.shard_map(
        per_device, mesh=finer, in_specs=in_specs, out_specs=out_specs, check_vma=False
    )
```

profile of v0, /device:TPU:4, one launch (start us, length us, event | category | flops | bytes accessed | tf_op | source)
XLA Modules:
  0.0 782.8 jit_solution(11673476122548457123)
XLA Ops:
  7.2 1.6 copy.290
  8.9 1.6 copy.289
  10.5 307.9 %all-gather.6.cloned.1.call-done = bf16[2,2560,2,192]{3,1,2,0:T(8,128)(2,1)} async-done(((bf16[2,40,2,192]{3,1,2,0:T(8,128)(2,1)}), bf16[2,2560,2,192]{3,1,2,0:T(8,128)(2,1)}) %all-gather.6.cloned.1.call-update) | async-done | bytes 3932176 | tf_op jit(solution)/shard_map/all_gather | solution.py:117
  318.5 3.5 fusion
  322.2 1.0 broadcast_in_dim.8
  323.2 4.8 all-to-all-start
  328.0 0.8 multiply_reduce_fusion.2
  328.8 12.3 %all-to-all-done = f32[4,2,40,2,192]{4,1,2,3,0:T(2,128)S(1)} async-done(((f32[4,2,40,2,192]{4,1,2,3,0:T(2,128)}), f32[4,2,40,2,192]{4,1,2,3,0:T(2,128)S(1)}, u32[]{:S(2)}, u32[]{:S(2)}) %all-to-all-start) | async-done | bytes 491552 | tf_op jit(solution)/shard_map/all_to_all | solution.py:27
  341.8 2.4 fusion.7
  344.1 2.5 add_select_fusion.1
  346.7 1.4 fusion.115
  348.1 1.4 fusion.105
  349.5 2.4 fusion.8
  351.8 2.5 subtract_select_fusion.1
  354.4 1.6 fusion.103
  355.9 1.4 fusion.117
  357.4 0.6 multiply_reduce_fusion.1
  358.0 7.1 all-reduce.4
  365.1 3.1 all-reduce.3
  368.1 8.3 %all-reduce.1 = (f32[]{:T(128)}, f32[]{:T(128)}) all-reduce(f32[]{:T(128)} %get-tuple-element.38, f32[]{:T(128)} %get-tuple-element.39), channel_id=1, replica_groups=mesh['freq_0'=2,'freq_1'=2,'rcv_0'=4,'rcv_1'=8,'rcv_2'=2] {'rcv_0'}, use_global_device_ids=true, to_apply=%region_3.0 | all-reduce | flops 2 | bytes 16 | tf_op jit(solution)/shard_map/psum | solution.py:38
  376.5 20.8 %all-reduce = (f32[]{:T(128)}, f32[]{:T(128)}) all-reduce(f32[]{:T(128)} %get-tuple-element.34, f32[]{:T(128)} %get-tuple-element.35), channel_id=1, replica_groups=mesh['freq_0'=2,'freq_1'=2,'rcv_0'=4,'rcv_1'=8,'rcv_2'=2] {'rcv_1'}, use_global_device_ids=true, to_apply=%region_4.0 | all-reduce | flops 2 | bytes 16 | tf_op jit(solution)/shard_map/psum | solution.py:38
  397.3 5.8 all-reduce.2
  404.5 0.7 copy-done.5
  405.4 18.5 %all_to_all.20 = f32[4,2,40,2,192]{4,1,2,3,0:T(2,128)S(1)} all-to-all(f32[4,2,40,2,192]{4,1,2,3,0:T(2,128)S(1)} %broadcast_in_dim.9), channel_id=1, replica_groups=mesh['freq_0'=2,'freq_1'=2,'rcv_0'=4,'rcv_1'=8,'rcv_2'=2] {'freq_0','fre..., dimensions={0} | all-to-all | bytes 983040 | tf_op jit(solution)/shard_map/all_to_all | solution.py:27
  424.6 2.4 fusion.10
  427.0 2.5 subtract_select_fusion
  429.5 1.4 fusion.99
  430.9 2.4 fusion.9
  433.3 2.5 add_select_fusion
  435.8 1.4 fusion.111
  437.2 1.8 fusion.101
  439.0 1.4 fusion.113
  440.4 6.1 all_gather.23
  446.6 15.6 %all-gather = bf16[8,2,40,2,192]{4,2,3,1,0:T(8,128)(2,1)} all-gather(bf16[2,2,40,2,192]{4,2,3,1,0:T(8,128)(2,1)S(1)} %all_gather.23), channel_id=2, replica_groups=mesh['freq_0'=2,'freq_1'=2,'rcv_0'=4,'rcv_1'=8,'rcv_2'=2] {'rcv_0'}, dimensions={0}, use_global_device_ids=true | all-gather | bytes 614400 | tf_op jit(solution)/shard_map/all_gather | solution.py:45
  462.2 162.9 %all-gather.8.cloned.1.call-done = bf16[2,2560,2,192]{3,1,2,0:T(8,128)(2,1)} async-done(((bf16[2,40,2,192]{3,1,2,0:T(8,128)(2,1)}), bf16[2,2560,2,192]{3,1,2,0:T(8,128)(2,1)}) %all-gather.8.cloned.1.call-update) | async-done | bytes 3932176 | tf_op jit(solution)/shard_map/all_gather | solution.py:132
  625.1 3.5 fusion.2
  628.8 1.0 broadcast_in_dim.10
  629.8 4.8 all-to-all-start.2
  635.3 7.9 %all-to-all-done.2 = f32[4,2,40,2,192]{4,1,2,3,0:T(2,128)S(1)} async-done(((f32[4,2,40,2,192]{4,1,2,3,0:T(2,128)}), f32[4,2,40,2,192]{4,1,2,3,0:T(2,128)S(1)}, u32[]{:S(2)}, u32[]{:S(2)}) %all-to-all-start.2) | async-done | bytes 491552 | tf_op jit(solution)/shard_map/all_to_all | solution.py:27
  643.9 2.4 fusion.11
  646.3 3.9 fusion.12
  650.1 3.7 add_multiply_fusion
  653.8 34.5 %all-gather.10.cloned.1.call-done = bf16[32,2,2,40,2,192]{5,3,4,2,1,0:T(8,128)(2,1)} async-done(((bf16[4,2,2,40,2,192]{5,3,4,2,1,0:T(8,128)(2,1)}), bf16[32,2,2,40,2,192]{5,3,4,2,1,0:T(8,128)(2,1)}) %all-gather.10.cloned.1.call-update) | async-done | bytes 3932176 | tf_op jit(solution)/shard_map/all_gather | solution.py:45
  688.3 3.0 copy.180
  691.4 1.0 convolution_bitcast_fusion
  694.3 4.3 subtract_multiply_fusion
  698.6 7.1 psum.115
  705.7 3.8 fusion.109
  709.4 3.3 psum.116
  712.7 3.7 fusion.95
  716.4 11.1 %psum.117 = f32[]{:T(128)} all-reduce(f32[]{:T(128)} %psum.116), channel_id=1, replica_groups=mesh['freq_0'=2,'freq_1'=2,'rcv_0'=4,'rcv_1'=8,'rcv_2'=2] {'rcv_0'}, use_global_device_ids=true, to_apply=%region_15.0 | all-reduce | flops 1 | bytes 8 | tf_op jit(solution)/shard_map/psum | solution.py:38
  727.5 2.0 fusion.97
  729.5 16.1 %psum.118 = f32[]{:T(128)} all-reduce(f32[]{:T(128)} %psum.117), channel_id=1, replica_groups=mesh['freq_0'=2,'freq_1'=2,'rcv_0'=4,'rcv_1'=8,'rcv_2'=2] {'rcv_1'}, use_global_device_ids=true, to_apply=%region_16.0 | all-reduce | flops 1 | bytes 8 | tf_op jit(solution)/shard_map/psum | solution.py:38
  745.7 2.0 fusion.107
  747.7 5.5 psum.119
  753.9 1.1 multiply_add_fusion
  755.0 1.1 add_reduce_fusion
  756.1 0.8 broadcast_in_dim.11
  756.9 7.5 all-to-all-start.3
  764.3 1.7 copy.198
  766.0 0.8 copy.197
  766.8 0.8 copy.199
  767.6 0.8 copy.200
  768.4 6.9 all-to-all-done.3
  (58 shorter events, 5.5 us)
Async XLA Ops:
  7.2 311.3 %copy-start = (bf16[2,2,40,2560]{3,2,1,0:T(8,128)(2,1)S(1)}, bf16[2,2,40,2560]{3,2,1,0:T(8,128)(2,1)}, u32[]{:S(2)}) copy-start(bf16[2,2,40,2560]{3,2,1,0:T(8,128)(2,1)} %param.6) | copy-start | bytes 2457604
  7.2 311.3 %all-gather.6.cloned.1.call-start = ((), (), s32[]{:S(2)}) async-start(), calls=%async_computation.4 | async-start | bytes 5324800 | tf_op jit(solution)/shard_map/all_gather | solution.py:117
  8.9 616.2 %all-gather.8.cloned.1.call-start = ((), (), s32[]{:S(2)}) async-start(), calls=%async_computation.5 | async-start | bytes 5324800 | tf_op jit(solution)/shard_map/all_gather | solution.py:132
  322.0 6.0 copy-start.8
  323.2 17.9 %all-to-all-start = ((f32[4,2,40,2,192]{4,1,2,3,0:T(2,128)}), f32[4,2,40,2,192]{4,1,2,3,0:T(2,128)S(1)}, u32[]{:S(2)}, u32[]{:S(2)}) async-start(f32[4,2,40,2,192]{4,1,2,3,0:T(2,128)} %broadcast_in_dim.8), calls=%async_computation | async-start | bytes 1310720 | tf_op jit(solution)/shard_map/all_to_all | solution.py:27
  328.0 360.4 %all-gather.10.cloned.1.call-start = ((), (), s32[]{:S(2)}) async-start(), calls=%async_computation.6 | async-start | bytes 5898240 | tf_op jit(solution)/shard_map/all_gather | solution.py:45
  328.8 15.4 %copy-start.4 = (s32[40,192]{1,0:T(8,128)S(1)}, s32[40,192]{1,0:T(8,128)}, u32[]{:S(2)}) copy-start(s32[40,192]{1,0:T(8,128)} %param.7) | copy-start | bytes 92164
  354.4 50.0 %copy-start.9 = (f32[2,40,2,192]{3,2,1,0:T(2,128)S(1)}, f32[2,40,2,192]{3,2,1,0:T(2,128)}, u32[]{:S(2)}) copy-start(f32[2,40,2,192]{3,2,1,0:T(2,128)} %param.9) | copy-start | bytes 368644
  404.4 0.7 copy-start.5
  629.8 13.4 %all-to-all-start.2 = ((f32[4,2,40,2,192]{4,1,2,3,0:T(2,128)}), f32[4,2,40,2,192]{4,1,2,3,0:T(2,128)S(1)}, u32[]{:S(2)}, u32[]{:S(2)}) async-start(f32[4,2,40,2,192]{4,1,2,3,0:T(2,128)} %broadcast_in_dim.10), calls=%async_computation.2 | async-start | bytes 1310720 | tf_op jit(solution)/shard_map/all_to_all | solution.py:27
  643.9 2.4 copy-start.2
  691.4 3.0 copy-start.1
  691.4 3.0 copy-start.3
  692.4 0.6 copy-start.6
  693.1 0.6 copy-start.7
  756.9 18.5 %all-to-all-start.3 = ((f32[64,2,2,192]{3,2,1,0:T(2,128)}), f32[64,2,2,192]{3,2,1,0:T(2,128)S(1)}, u32[]{:S(2)}, u32[]{:S(2)}) async-start(f32[64,2,2,192]{3,2,1,0:T(2,128)} %broadcast_in_dim.11), calls=%async_computation.3 | async-start | bytes 524288 | tf_op jit(solution)/shard_map/all_to_all | solution.py:27
Sparse Core Ops, SparseCore 0:
  10.4 308.0 all-gather.5
  320.8 304.2 all-gather.7
  626.9 61.3 all-gather.9
where the time goes:
time: 793 us; the launch traced here: 783 us
  waiting for transfers between devices  533 us (67%)
  blocking collectives  128 us (16%)
  matrix products  65.1 us (8%)
  local copies, waits for them, and re-layouts  17.5 us (2%)
  starting transfers between devices  17.1 us (2%)
  between operations  16.9 us (2%)
    all_gather x1, waiting for transfers between devices, per_device(): lax.all_gather(direction_low, RCV, axis=1, tiled=True)  308 us
    all_gather x1, waiting for transfers between devices, per_device(): lax.all_gather(focusing_low, RCV, axis=1, tiled=True)  163 us
    psum x10, blocking collectives, one_axis_at_a_time(): value = lax.psum(value, axis)  88.1 us
    all_gather x1, waiting for transfers between devices, all_blocks(): pieces = lax.all_gather(pieces, axes[k])  34.5 us
    dot_general x12, matrix products, contract_time(): return jnp.einsum('tf,frk->trk', table, values, precision=highest)  33.8 us
    all_to_all x3, waiting for transfers between devices, sent_to_all(): lax.all_to_all(jnp.broadcast_to(value[None], (count, *value.shape)), axis...  27.2 us
    dot_general x12, matrix products, contract_back(): return jnp.einsum('tf,trk->frk', table, values, precision=highest)  23.2 us
    all_gather x2, blocking collectives, all_blocks(): pieces = lax.all_gather(pieces, axes[k])  21.7 us
  transfers between devices with their start and end apart: 6, of which 6 were waited for; matrix products, arithmetic and copies ran while one was open for 8% of the time, Pallas kernels for 0%

commit v1 on v0

--- a/solution.py
+++ b/solution.py
@@ -129,7 +129,11 @@
     new_gradient = combine(total, True)
     new_gamma = one_axis_at_a_time(jnp.sum(new_gradient * new_gradient), FREQ_RCV)
     new_direction = new_gradient + new_gamma / (gamma + tiny) * direction
-    focus_total = accumulate(lax.all_gather(focusing_low, RCV, axis=1, tiled=True))
+    focus_total = accumulate(
+        jnp.concatenate(
+            lax.all_to_all(jnp.stack([focusing_low] * lax.axis_size(RCV)), RCV, 0, 0), axis=1
+        )
+    )
     focusing_image = combine(focus_total, False)
     green_field = gate(focusing_image + alpha * direction_image, True)
     corr_real = jnp.sum(

time: 793 us -> 707 us (0.89)
  waiting for transfers between devices: 533 us -> 448 us
  blocking collectives: 128 us -> 110 us
  starting transfers between devices: 17.1 us -> 30.8 us
    all_gather x1 -> x0, waiting for transfers between devices: 163 us -> none  [per_device(): lax.all_gather(focusing_low, RCV, axis=1, tiled=True)]
    all_to_all x0 -> x1, waiting for transfers between devices: none -> 107 us  [per_device(): lax.all_to_all(jnp.stack([focusing_low] * lax.axis_size(RCV)), RCV, 0, 0)]
    all_gather x1, waiting for transfers between devices: 34.5 us -> 0.02 us  [all_blocks(): pieces = lax.all_gather(pieces, axes[k])]
    all_to_all x1 -> x0, blocking collectives: 18.5 us -> none  [sent_to_all(): lax.all_to_all(jnp.broadcast_to(value[None], (count, *value.shape)), axis...]
    all_to_all x3 -> x4, starting transfers between devices: 17 us -> 25 us  [sent_to_all(): lax.all_to_all(jnp.broadcast_to(value[None], (count, *value.shape)), axis...]
    all_to_all x3 -> x4, waiting for transfers between devices: 27.2 us -> 31.2 us  [sent_to_all(): lax.all_to_all(jnp.broadcast_to(value[None], (count, *value.shape)), axis...]
  transfers between devices with their start and end apart: 6 -> 7, of which waited for: 6 -> 6; matrix products, arithmetic and copies ran while one was open for 8% -> 5% of each run, Pallas kernels for 0% -> 0%
where the time goes in v1:
time: 707 us; the launch traced here: 695 us
  waiting for transfers between devices  448 us (63%)
  blocking collectives  110 us (16%)
  matrix products  60.8 us (9%)
  starting transfers between devices  30.8 us (4%)
  local copies, waits for them, and re-layouts  22.7 us (3%)
  between operations  17.3 us (2%)
    all_gather x1, waiting for transfers between devices, per_device(): lax.all_gather(direction_low, RCV, axis=1, tiled=True)  310 us
    all_to_all x1, waiting for transfers between devices, per_device(): lax.all_to_all(jnp.stack([focusing_low] * lax.axis_size(RCV)), RCV, 0, 0)  107 us
    psum x10, blocking collectives, one_axis_at_a_time(): value = lax.psum(value, axis)  85.5 us
    dot_general x12, matrix products, contract_time(): return jnp.einsum('tf,frk->trk', table, values, precision=highest)  33.7 us
    all_to_all x4, waiting for transfers between devices, sent_to_all(): lax.all_to_all(jnp.broadcast_to(value[None], (count, *value.shape)), axis...  31.2 us
    all_to_all x4, starting transfers between devices, sent_to_all(): lax.all_to_all(jnp.broadcast_to(value[None], (count, *value.shape)), axis...  25 us
    all_gather x2, blocking collectives, all_blocks(): pieces = lax.all_gather(pieces, axes[k])  24.4 us
    dot_general x12, matrix products, contract_back(): return jnp.einsum('tf,trk->frk', table, values, precision=highest)  21.5 us
  transfers between devices with their start and end apart: 7, of which 6 were waited for; matrix products, arithmetic and copies ran while one was open for 5% of the time, Pallas kernels for 0%

profile of v1, /device:TPU:4, one launch (start us, length us, event | category | flops | bytes accessed | tf_op | source)
XLA Modules:
  0.0 694.8 jit_solution(7637433733397216360)
XLA Ops:
  7.2 1.6 copy.297
  8.9 309.6 %all-gather.5.cloned.1.call-done = bf16[2,2560,2,192]{3,1,2,0:T(8,128)(2,1)} async-done(((bf16[2,40,2,192]{3,1,2,0:T(8,128)(2,1)}), bf16[2,2560,2,192]{3,1,2,0:T(8,128)(2,1)}) %all-gather.5.cloned.1.call-update) | async-done | bytes 3932176 | tf_op jit(solution)/shard_map/all_gather | solution.py:117
  318.5 3.5 fusion
  322.2 1.0 broadcast_in_dim.8
  323.2 4.8 all-to-all-start
  328.0 0.8 multiply_reduce_fusion.2
  328.8 7.8 %all-to-all-done = f32[4,2,40,2,192]{4,1,2,3,0:T(2,128)S(1)} async-done(((f32[4,2,40,2,192]{4,1,2,3,0:T(2,128)}), f32[4,2,40,2,192]{4,1,2,3,0:T(2,128)S(1)}, u32[]{:S(2)}, u32[]{:S(2)}) %all-to-all-start) | async-done | bytes 491552 | tf_op jit(solution)/shard_map/all_to_all | solution.py:27
  337.2 2.4 fusion.7
  339.6 2.5 add_select_fusion.1
  342.2 1.4 fusion.105
  343.5 1.4 fusion.115
  344.9 2.4 fusion.8
  347.3 2.5 subtract_select_fusion.1
  349.8 1.6 fusion.117
  351.4 1.4 fusion.103
  353.5 7.1 %all-reduce.4 = (f32[]{:T(128)}, f32[]{:T(128)}) all-reduce(f32[]{:T(128)} %multiply_reduce_fusion.2, f32[]{:T(128)} %multiply_reduce_fusion.1), channel_id=1, replica_groups=mesh['freq_0'=2,'freq_1'=2,'rcv_0'=4,'rcv_1'=8,'rcv_2'=2] {'freq_0'}, use_global_device_ids=true, to_apply=%region_1.0 | all-reduce | flops 2 | bytes 16 | tf_op jit(solution)/shard_map/psum | solution.py:38
  360.5 3.1 all-reduce.3
  363.6 8.3 %all-reduce.1 = (f32[]{:T(128)}, f32[]{:T(128)}) all-reduce(f32[]{:T(128)} %get-tuple-element.38, f32[]{:T(128)} %get-tuple-element.39), channel_id=1, replica_groups=mesh['freq_0'=2,'freq_1'=2,'rcv_0'=4,'rcv_1'=8,'rcv_2'=2] {'rcv_0'}, use_global_device_ids=true, to_apply=%region_3.0 | all-reduce | flops 2 | bytes 16 | tf_op jit(solution)/shard_map/psum | solution.py:38
  372.0 19.8 %all-reduce = (f32[]{:T(128)}, f32[]{:T(128)}) all-reduce(f32[]{:T(128)} %get-tuple-element.34, f32[]{:T(128)} %get-tuple-element.35), channel_id=1, replica_groups=mesh['freq_0'=2,'freq_1'=2,'rcv_0'=4,'rcv_1'=8,'rcv_2'=2] {'rcv_1'}, use_global_device_ids=true, to_apply=%region_4.0 | all-reduce | flops 2 | bytes 16 | tf_op jit(solution)/shard_map/psum | solution.py:38
  391.7 5.5 all-reduce.2
  399.4 1.0 broadcast_in_dim.9
  400.4 6.6 all-to-all-start.1
  407.1 8.5 %all-to-all-done.1 = f32[4,2,40,2,192]{4,1,2,3,0:T(2,128)S(1)} async-done(((f32[4,2,40,2,192]{4,1,2,3,0:T(2,128)}), f32[4,2,40,2,192]{4,1,2,3,0:T(2,128)S(1)}, u32[]{:S(2)}, u32[]{:S(2)}) %all-to-all-start.1) | async-done | bytes 491552 | tf_op jit(solution)/shard_map/all_to_all | solution.py:27
  415.6 3.0 stack.40
  418.6 5.7 all-to-all-start.2
  425.0 2.3 fusion.9
  427.4 2.5 add_select_fusion
  429.9 1.4 fusion.101
  431.3 2.4 fusion.10
  433.6 2.5 subtract_select_fusion
  436.2 1.4 fusion.113
  437.6 1.8 fusion.111
  439.4 1.4 fusion.99
  440.8 7.3 %all_gather.20 = bf16[2,2,40,2,192]{4,2,3,1,0:T(8,128)(2,1)S(1)} all-gather(bf16[1,2,40,2,192]{4,2,3,1,0:T(8,128)(2,1)S(1)} %copy.184), channel_id=1, replica_groups=mesh['freq_0'=2,'freq_1'=2,'rcv_0'=4,'rcv_1'=8,'rcv_2'=2] {'rcv_2'}, dimensions={0}, use_global_device_ids=true | all-gather | bytes 184320 | tf_op jit(solution)/shard_map/all_gather | solution.py:45
  448.1 17.1 %all-gather = bf16[8,2,40,2,192]{4,2,3,1,0:T(8,128)(2,1)} all-gather(bf16[2,2,40,2,192]{4,2,3,1,0:T(8,128)(2,1)S(1)} %all_gather.20), channel_id=2, replica_groups=mesh['freq_0'=2,'freq_1'=2,'rcv_0'=4,'rcv_1'=8,'rcv_2'=2] {'rcv_0'}, dimensions={0}, use_global_device_ids=true | all-gather | bytes 614400 | tf_op jit(solution)/shard_map/all_gather | solution.py:45
  465.2 107.4 %all-to-all-done.2 = bf16[64,2,40,2,192]{4,2,3,1,0:T(8,128)(2,1)} async-done(((bf16[64,2,40,2,192]{4,2,3,1,0:T(8,128)(2,1)}), bf16[64,2,40,2,192]{4,2,3,1,0:T(8,128)(2,1)}, u32[]{:S(2)}, u32[]{:S(2)}) %all-to-all-start.2) | async-done | bytes 3932192 | tf_op jit(solution)/shard_map/all_to_all | solution.py:134
  572.6 2.9 copy.191
  575.5 1.0 fusion.2
  576.7 1.0 broadcast_in_dim.10
  577.8 7.2 %all-to-all-start.3 = ((f32[4,2,40,2,192]{4,1,2,3,0:T(2,128)}), f32[4,2,40,2,192]{4,1,2,3,0:T(2,128)S(1)}, u32[]{:S(2)}, u32[]{:S(2)}) async-start(f32[4,2,40,2,192]{4,1,2,3,0:T(2,128)} %broadcast_in_dim.10), calls=%async_computation.3 | async-start | bytes 1310720 | tf_op jit(solution)/shard_map/all_to_all | solution.py:27
  585.6 7.9 %all-to-all-done.3 = f32[4,2,40,2,192]{4,1,2,3,0:T(2,128)S(1)} async-done(((f32[4,2,40,2,192]{4,1,2,3,0:T(2,128)}), f32[4,2,40,2,192]{4,1,2,3,0:T(2,128)S(1)}, u32[]{:S(2)}, u32[]{:S(2)}) %all-to-all-start.3) | async-done | bytes 491552 | tf_op jit(solution)/shard_map/all_to_all | solution.py:27
  594.2 2.4 fusion.12
  596.6 3.9 fusion.11
  600.5 3.7 subtract_multiply_fusion
  604.2 3.0 copy.185
  607.2 1.0 convolution_bitcast_fusion
  610.2 4.3 add_multiply_fusion
  614.5 7.1 %psum.115 = f32[]{:T(128)} all-reduce(f32[]{:T(128)} %multiply_reduce_fusion), channel_id=1, replica_groups=mesh['freq_0'=2,'freq_1'=2,'rcv_0'=4,'rcv_1'=8,'rcv_2'=2] {'freq_0'}, use_global_device_ids=true, to_apply=%region_13.0 | all-reduce | flops 1 | bytes 8 | tf_op jit(solution)/shard_map/psum | solution.py:38
  621.5 2.0 fusion.95
  623.6 3.3 psum.116
  626.8 2.0 fusion.109
  628.8 9.5 %psum.117 = f32[]{:T(128)} all-reduce(f32[]{:T(128)} %psum.116), channel_id=1, replica_groups=mesh['freq_0'=2,'freq_1'=2,'rcv_0'=4,'rcv_1'=8,'rcv_2'=2] {'rcv_0'}, use_global_device_ids=true, to_apply=%region_15.0 | all-reduce | flops 1 | bytes 8 | tf_op jit(solution)/shard_map/psum | solution.py:38
  638.3 3.8 fusion.107
  642.1 14.8 %psum.118 = f32[]{:T(128)} all-reduce(f32[]{:T(128)} %psum.117), channel_id=1, replica_groups=mesh['freq_0'=2,'freq_1'=2,'rcv_0'=4,'rcv_1'=8,'rcv_2'=2] {'rcv_1'}, use_global_device_ids=true, to_apply=%region_16.0 | all-reduce | flops 1 | bytes 8 | tf_op jit(solution)/shard_map/psum | solution.py:38
  656.9 2.0 fusion.97
  658.9 7.1 %psum.119 = f32[]{:T(128)} all-reduce(f32[]{:T(128)} %psum.118), channel_id=1, replica_groups=mesh['freq_0'=2,'freq_1'=2,'rcv_0'=4,'rcv_1'=8,'rcv_2'=2] {'rcv_2'}, use_global_device_ids=true, to_apply=%region_17.0 | all-reduce | flops 1 | bytes 8 | tf_op jit(solution)/shard_map/psum | solution.py:38
  666.7 1.1 multiply_add_fusion
  667.8 1.1 add_reduce_fusion
  669.6 6.4 all-to-all-start.4
  676.0 1.7 copy.205
  677.7 0.8 copy.204
  678.6 0.8 copy.207
  679.3 0.8 copy.206
  680.1 6.9 all-to-all-done.4
  (67 shorter events, 7.5 us)
Async XLA Ops:
  7.2 311.3 %copy-start = (bf16[2,2,40,2560]{3,2,1,0:T(8,128)(2,1)S(1)}, bf16[2,2,40,2560]{3,2,1,0:T(8,128)(2,1)}, u32[]{:S(2)}) copy-start(bf16[2,2,40,2560]{3,2,1,0:T(8,128)(2,1)} %param.6) | copy-start | bytes 2457604
  7.2 311.3 %all-gather.5.cloned.1.call-start = ((), (), s32[]{:S(2)}) async-start(), calls=%async_computation.5 | async-start | bytes 5324800 | tf_op jit(solution)/shard_map/all_gather | solution.py:117
  322.0 6.0 copy-start.11
  323.2 13.4 %all-to-all-start = ((f32[4,2,40,2,192]{4,1,2,3,0:T(2,128)}), f32[4,2,40,2,192]{4,1,2,3,0:T(2,128)S(1)}, u32[]{:S(2)}, u32[]{:S(2)}) async-start(f32[4,2,40,2,192]{4,1,2,3,0:T(2,128)} %broadcast_in_dim.8), calls=%async_computation | async-start | bytes 1310720 | tf_op jit(solution)/shard_map/all_to_all | solution.py:27
  328.8 10.8 %copy-start.5 = (s32[40,192]{1,0:T(8,128)S(1)}, s32[40,192]{1,0:T(8,128)}, u32[]{:S(2)}) copy-start(s32[40,192]{1,0:T(8,128)} %param.7) | copy-start | bytes 92164
  349.8 48.8 %copy-start.12 = (f32[2,40,2,192]{3,2,1,0:T(2,128)S(1)}, f32[2,40,2,192]{3,2,1,0:T(2,128)}, u32[]{:S(2)}) copy-start(f32[2,40,2,192]{3,2,1,0:T(2,128)} %param.9) | copy-start | bytes 368644
  351.4 55.6 %copy-start.10 = (f32[2,40,2,192]{3,2,1,0:T(2,128)S(1)}, f32[2,40,2,192]{3,2,1,0:T(2,128)}, u32[]{:S(2)}) copy-start(f32[2,40,2,192]{3,2,1,0:T(2,128)} %param.8) | copy-start | bytes 368644
  398.6 0.7 copy-start.6
  400.4 15.2 %all-to-all-start.1 = ((f32[4,2,40,2,192]{4,1,2,3,0:T(2,128)}), f32[4,2,40,2,192]{4,1,2,3,0:T(2,128)S(1)}, u32[]{:S(2)}, u32[]{:S(2)}) async-start(f32[4,2,40,2,192]{4,1,2,3,0:T(2,128)} %broadcast_in_dim.9), calls=%async_computation.1 | async-start | bytes 1310720 | tf_op jit(solution)/shard_map/all_to_all | solution.py:27
  418.6 154.1 %all-to-all-start.2 = ((bf16[64,2,40,2,192]{4,2,3,1,0:T(8,128)(2,1)}), bf16[64,2,40,2,192]{4,2,3,1,0:T(8,128)(2,1)}, u32[]{:S(2)}, u32[]{:S(2)}) async-start(bf16[64,2,40,2,192]{4,2,3,1,0:T(8,128)(2,1)} %stack.40), calls=%async_computation.2 | async-start | bytes 10485760 | tf_op jit(solution)/shard_map/all_to_all | solution.py:134
  424.3 179.9 %all-gather.7.cloned.1.call-start = ((), (), s32[]{:S(2)}) async-start(), calls=%async_computation.6 | async-start | bytes 5898240 | tf_op jit(solution)/shard_map/all_gather | solution.py:45
  577.8 15.8 %all-to-all-start.3 = ((f32[4,2,40,2,192]{4,1,2,3,0:T(2,128)}), f32[4,2,40,2,192]{4,1,2,3,0:T(2,128)S(1)}, u32[]{:S(2)}, u32[]{:S(2)}) async-start(f32[4,2,40,2,192]{4,1,2,3,0:T(2,128)} %broadcast_in_dim.10), calls=%async_computation.3 | async-start | bytes 1310720 | tf_op jit(solution)/shard_map/all_to_all | solution.py:27
  594.2 2.4 copy-start.3
  607.2 3.0 copy-start.2
  607.2 3.0 copy-start.4
  608.3 0.6 copy-start.7
  608.9 0.6 copy-start.9
  628.8 28.1 %copy-start.1 = (f32[64,40,192]{2,0,1:T(8,128)S(1)}, f32[64,40,192]{2,0,1:T(8,128)}, u32[]{:S(2)}) copy-start(f32[64,40,192]{2,0,1:T(8,128)} %add_multiply_fusion) | copy-start | bytes 5898244
  638.3 28.4 %copy-start.8 = (f32[2,40,1,192]{3,1,0,2:T(8,128)S(1)}, f32[2,40,1,192]{3,1,0,2:T(8,128)}, u32[]{:S(2)}) copy-start(f32[2,40,1,192]{3,1,0,2:T(8,128)} %copy-done.7) | copy-start | bytes 184324
  669.6 17.5 %all-to-all-start.4 = ((f32[64,2,2,192]{3,2,1,0:T(2,128)}), f32[64,2,2,192]{3,2,1,0:T(2,128)S(1)}, u32[]{:S(2)}, u32[]{:S(2)}) async-start(f32[64,2,2,192]{3,2,1,0:T(2,128)} %broadcast_in_dim.11), calls=%async_computation.4 | async-start | bytes 524288 | tf_op jit(solution)/shard_map/all_to_all | solution.py:27
Sparse Core Ops, SparseCore 0:
  10.4 308.0 all-gather.4
  465.3 123.8 all-gather.6
